TPU v7x, 32 devices: a whole 2x2x4 slice. The times are simulated.
32 devices in a mesh: section: 4 (over z), dp: 2 (over x), mp: 4 (over y, core).
Axes of the slice: x: 2, y: 2, z: 4, core: 2. Of those that a mesh axis runs over, the one named last changes fastest.
Arguments:
- entrance: bfloat16 [2, 2, 96, 4096], P('dp'), may hold values from -6 to 6
- lengths: int32 [2, 2], P('dp'), may hold values from 24 to 96
- positives: int32 [2], replicated, may hold values from 0 to 1, each once
- norm_gains: float32 [4, 4096], P('section'), may hold values from 0.5 to 1.5
- query_proj: bfloat16 [4, 4096, 2048], P('section', None, 'mp'), may hold values from -0.09375 to 0.09375
- key_proj: bfloat16 [4, 4096, 512], P('section', None, 'mp'), may hold values from -0.09375 to 0.09375
- value_proj: bfloat16 [4, 4096, 512], P('section', None, 'mp'), may hold values from -0.09375 to 0.09375
- out_proj: bfloat16 [4, 2048, 4096], P('section', 'mp'), may hold values from -0.125 to 0.125
Outputs:
- losses: float32 [4, 7], P('section')
- norm_gain_grad: float32 [4, 4096], P('section', ('dp', 'mp'))
- query_proj_grad: float32 [4, 4096, 2048], P('section', 'dp', 'mp')
- key_proj_grad: float32 [4, 4096, 512], P('section', 'dp', 'mp')
- value_proj_grad: float32 [4, 4096, 512], P('section', 'dp', 'mp')
- out_proj_grad: float32 [4, 2048, 4096], P('section', 'mp', 'dp')
Inputs may be any that keep to these rules, and one draw needn't show every extreme that they name: positives is a permutation of the pair indices. `lengths`: tokens at or past a sequence's length are padding.
All inputs are finite; a program needn't handle non-finite values.
Results may differ from a plain program's by a relative error of at most 0.039.
Values may be sent and summed in bfloat16 or wider, within the bound.
A program may use at most 128 MiB of HBM per device.

v0:
```python
import jax
import jax.numpy as jnp
from jax import lax
from jax.sharding import PartitionSpec as P

HEAD = 128
WIDTHS = 7


EPSILON = 1e-05
SOFTMAX_TEMPER = 0.05
ROPE_BASE = 500000.0


def passed_along(value, axis, steps):
    count = lax.axis_size(axis)
    first, last = (max(0, -steps), min(count, count - steps))
    return lax.ppermute(value, axis, [(source, source + steps) for source in range(first, last)])


def rope_tables(length, head_size):
    half_size = head_size // 2
    inverse_freq = ROPE_BASE ** (-jnp.arange(half_size, dtype=jnp.float32) * 2.0 / head_size)
    angles = jnp.arange(length, dtype=jnp.float32)[:, None] * inverse_freq[None, :]
    return (jnp.cos(angles), jnp.sin(angles))


def rotate(values, cosine, sine_table):
    half_size = values.shape[-1] // 2
    first_half = values[..., :half_size]
    second = values[..., half_size:]
    cosine = cosine[None, :, None, :]
    sine_table = sine_table[None, :, None, :]
    return jnp.concatenate(
        [first_half * cosine - second * sine_table, second * cosine + first_half * sine_table],
        axis=-1,
    )


def attend(query_pre, key_pre, value_pre):
    seq_count, length, query_width = query_pre.shape
    query_heads = query_width // HEAD
    kv_heads = key_pre.shape[-1] // HEAD
    group_size = query_heads // kv_heads
    cosine, sine_table = rope_tables(length, HEAD)
    query_vectors = rotate(
        query_pre.reshape(seq_count, length, query_heads, HEAD), cosine, sine_table
    ).astype(jnp.bfloat16)
    key_rows = rotate(
        key_pre.reshape(seq_count, length, kv_heads, HEAD), cosine, sine_table
    ).astype(jnp.bfloat16)
    values = value_pre.reshape(seq_count, length, kv_heads, HEAD).astype(jnp.bfloat16)
    query_vectors = query_vectors.reshape(seq_count, length, kv_heads, group_size, HEAD)
    scores = jnp.einsum(
        "sikge,sjke->skgij", query_vectors.astype(jnp.float32), key_rows.astype(jnp.float32)
    ) * HEAD ** (-0.5)
    causal = (
        jnp.arange(length, dtype=jnp.int32)[:, None] >= jnp.arange(length, dtype=jnp.int32)[None, :]
    )
    scores = jnp.where(causal, scores, -1e30)
    weights = jax.nn.softmax(scores, axis=-1).astype(jnp.bfloat16)
    mixture = jnp.einsum(
        "skgij,sjke->sikge", weights.astype(jnp.float32), values.astype(jnp.float32)
    )
    return mixture.reshape(seq_count, length, query_heads * HEAD)


def normalize(hidden_f, gain_vector):
    inv_rms = lax.rsqrt(jnp.mean(hidden_f * hidden_f, axis=-1, keepdims=True) + EPSILON)
    return hidden_f * inv_rms * gain_vector


def contract_rows(left, right):
    return lax.dot_general(
        left, right, (((0,), (0,)), ((), ())), preferred_element_type=jnp.float32
    )


def contract_last(left, right):
    return lax.dot_general(
        left, right, (((left.ndim - 1,), (1,)), ((), ())), preferred_element_type=jnp.float32
    )


def pool_exits(batch_rows, mask_of_valid, counts):
    total_value = jnp.einsum("ki,kiu->ku", mask_of_valid, batch_rows.astype(jnp.float32))
    return total_value / counts[:, None]


def spread_grad(exit_grad, mask_of_valid, counts):
    return mask_of_valid[:, :, None] * (exit_grad / counts[:, None])[:, None, :]


def matryoshka_losses(pooled, positives):
    pair_total = pooled.shape[0]
    target = (jnp.arange(pair_total, dtype=jnp.int32)[None, :] == positives[:, None]).astype(
        jnp.float32
    )
    losses = []
    for level_index in range(WIDTHS):
        leading_width = pooled.shape[-1] // 2**level_index
        query_vectors = pooled[:, 0, :leading_width]
        passage_rows = pooled[:, 1, :leading_width]
        query_vectors = query_vectors * lax.rsqrt(
            jnp.mean(query_vectors * query_vectors, axis=-1, keepdims=True) + 1e-06
        )
        passage_rows = passage_rows * lax.rsqrt(
            jnp.mean(passage_rows * passage_rows, axis=-1, keepdims=True) + 1e-06
        )
        score_matrix = jnp.dot(query_vectors, passage_rows.T, precision=lax.Precision.HIGHEST) / (
            leading_width * SOFTMAX_TEMPER
        )
        picked = jnp.sum(score_matrix * target, axis=-1)
        losses.append(jnp.mean(jax.nn.logsumexp(score_matrix, axis=-1) - picked))
    return jnp.stack(losses)


def pass_along(batch_rows, direction):
    return passed_along(batch_rows, "section", direction)


def forward_section(hidden, gain_vector, query_weight, key_weight, value_weight, out_weight):
    hidden_f = hidden.astype(jnp.float32)
    normed = normalize(hidden_f, gain_vector).astype(jnp.bfloat16)
    mixture = attend(
        jnp.dot(normed, query_weight, preferred_element_type=jnp.float32),
        jnp.dot(normed, key_weight, preferred_element_type=jnp.float32),
        jnp.dot(normed, value_weight, preferred_element_type=jnp.float32),
    ).astype(jnp.bfloat16)
    partial_value = jnp.dot(mixture, out_weight, preferred_element_type=jnp.float32)
    total_value = lax.psum(partial_value.astype(jnp.bfloat16), "mp").astype(jnp.float32)
    return (hidden_f + total_value).astype(jnp.bfloat16)


def backward_section(
    hidden, upstream, gain_vector, query_weight, key_weight, value_weight, out_weight
):
    hidden_f = hidden.astype(jnp.float32)
    inv_rms = lax.rsqrt(jnp.mean(hidden_f * hidden_f, axis=-1, keepdims=True) + EPSILON)
    normed = normalize(hidden_f, gain_vector).astype(jnp.bfloat16)
    out_grad = upstream.astype(jnp.bfloat16)
    mixture_f, pullback = jax.vjp(
        attend,
        jnp.dot(normed, query_weight, preferred_element_type=jnp.float32),
        jnp.dot(normed, key_weight, preferred_element_type=jnp.float32),
        jnp.dot(normed, value_weight, preferred_element_type=jnp.float32),
    )
    mixture = mixture_f.astype(jnp.bfloat16)
    mixture_grad = contract_last(out_grad, out_weight).astype(jnp.bfloat16)
    pulled = pullback(lax.optimization_barrier(mixture_grad).astype(jnp.float32))
    query_grad, key_grad, value_grad = [piece_grad.astype(jnp.bfloat16) for piece_grad in pulled]
    member_grad = (
        contract_last(query_grad, query_weight)
        + contract_last(key_grad, key_weight)
        + contract_last(value_grad, value_weight)
    )
    normed_grad = lax.psum(member_grad.astype(jnp.bfloat16), "mp").astype(jnp.float32)
    rounded = lax.optimization_barrier(member_grad.astype(jnp.bfloat16)).astype(jnp.float32)
    gain_term = jnp.sum(rounded * hidden_f * inv_rms, axis=(0, 1))
    _, norm_pull = jax.vjp(lambda values: normalize(values, gain_vector), hidden_f)
    input_grad = (upstream + norm_pull(normed_grad)[0]).astype(jnp.bfloat16)
    width_all = hidden.shape[-1]
    head_grads = jnp.concatenate([query_grad, key_grad, value_grad], axis=-1)
    stored_now = (
        normed.reshape(-1, width_all),
        out_grad.reshape(-1, width_all),
        head_grads.reshape(-1, head_grads.shape[-1]),
        mixture.reshape(-1, mixture.shape[-1]),
        gain_term,
    )
    return (input_grad, stored_now)


def local(entrance, lengths, positives, norm_gains, query_proj, key_proj, value_proj, out_proj):
    section_count = lax.axis_size("section")
    section_index = lax.axis_index("section")
    pair_count = entrance.shape[0]
    seq_count = 2 * pair_count
    length = entrance.shape[2]
    width_all = entrance.shape[3]
    start_hidden = entrance.reshape(seq_count, length, width_all)
    mask_of_valid = (
        jnp.arange(length, dtype=jnp.int32)[None, :] < lengths.reshape(seq_count, 1)
    ).astype(jnp.float32)
    counts = jnp.sum(mask_of_valid, axis=1)
    gain_vector = norm_gains[0]
    query_weight = query_proj[0]
    key_weight = key_proj[0]
    value_weight = value_proj[0]
    out_weight = out_proj[0]
    current = start_hidden
    saved_input = start_hidden
    exit_rows = start_hidden
    for section_turn in range(section_count):
        produced = forward_section(
            current, gain_vector, query_weight, key_weight, value_weight, out_weight
        )
        chosen = section_index == section_turn
        saved_input = jnp.where(chosen, current, saved_input)
        exit_rows = jnp.where(chosen, produced, exit_rows)
        if section_turn + 1 < section_count:
            arrived = pass_along(produced, 1)
            current = jnp.where(section_index == 0, start_hidden, arrived)
    pooled = pool_exits(exit_rows, mask_of_valid, counts).reshape(pair_count, 2, width_all)
    gathered = lax.all_gather(pooled.astype(jnp.bfloat16), "dp", axis=0, tiled=True).astype(
        pooled.dtype
    )
    losses_now, pullback = jax.vjp(
        lambda embedded: matryoshka_losses(embedded, positives), gathered
    )
    pair_grads = pullback(jnp.ones((WIDTHS,), jnp.float32))[0]
    own_losses = losses_now[None]
    own_grad = lax.dynamic_slice_in_dim(
        pair_grads, lax.axis_index("dp") * pair_count, pair_count, 0
    )
    token_grad = spread_grad(own_grad.reshape(seq_count, width_all), mask_of_valid, counts)
    incoming = jnp.zeros(start_hidden.shape, jnp.bfloat16)
    stored = None
    for section_turn in range(section_count):
        owner_section = section_count - 1 - section_turn
        upstream = token_grad + incoming.astype(jnp.float32)
        input_grad, stored_now = backward_section(
            saved_input, upstream, gain_vector, query_weight, key_weight, value_weight, out_weight
        )
        chosen = section_index == owner_section
        if stored is None:
            stored = stored_now
        else:
            stored = jax.tree.map(
                lambda fresh, former: jnp.where(chosen, fresh, former), stored_now, stored
            )
        if section_turn + 1 < section_count:
            incoming = pass_along(input_grad, -1)
    normed_rows, out_rows, head_grads, mixture_rows, gain_term = stored
    gain_share = lax.psum_scatter(gain_term, ("dp", "mp"), scatter_dimension=0, tiled=True)
    normed_cols, out_cols = (
        lax.all_to_all(normed_rows, "dp", split_axis=1, concat_axis=0, tiled=True),
        lax.all_to_all(out_rows, "dp", split_axis=1, concat_axis=0, tiled=True),
    )
    head_piece = lax.all_gather(head_grads, "dp", axis=0, tiled=True)
    mixture_piece = lax.all_gather(mixture_rows, "dp", axis=0, tiled=True)
    weight_sums = jnp.concatenate(
        [contract_rows(normed_cols, head_piece), contract_rows(out_cols, mixture_piece)], axis=1
    )
    query_cols = query_weight.shape[1]
    kv_cols = key_weight.shape[1]
    query_grad_out = weight_sums[:, :query_cols][None]
    key_grad_out = weight_sums[:, query_cols : query_cols + kv_cols][None]
    value_grad_out = weight_sums[:, query_cols + kv_cols : query_cols + 2 * kv_cols][None]
    out_grad_out = weight_sums[:, query_cols + 2 * kv_cols :].T[None]
    return (
        own_losses,
        gain_share[None],
        query_grad_out,
        key_grad_out,
        value_grad_out,
        out_grad_out,
    )


def solution(mesh):
    in_specs = (
        P("dp", None, None, None),
        P("dp", None),
        P(),
        P("section", None),
        P("section", None, "mp"),
        P("section", None, "mp"),
        P("section", None, "mp"),
        P("section", "mp", None),
    )
    out_specs = (
        P("section", None),
        P("section", ("dp", "mp")),
        P("section", "dp", "mp"),
        P("section", "dp", "mp"),
        P("section", "dp", "mp"),
        P("section", "mp", "dp"),
    )
    return jax.shard_map(local, mesh=mesh, in_specs=in_specs, out_specs=out_specs, check_vma=False)
```

profile of v0, /device:TPU:0, one launch (start us, length us, event | category | flops | bytes accessed | tf_op | source)
XLA Modules:
  0.0 794.6 jit_solution(6625503369172345784)
XLA Ops:
  9.4 6.4 copy.140
  27.7 45.7 %all-reduce.39.cloned.1.call-done = bf16[2,96,4096]{2,1,0:T(8,128)(2,1)} async-done(((bf16[2,96,4096]{2,1,0:T(8,128)(2,1)}), bf16[2,96,4096]{2,1,0:T(8,128)(2,1)}) %all-reduce.39.cloned.1.call-update) | async-done | bytes 1572880 | tf_op jit(solution)/shard_map/psum | solution.py:131
  76.5 4.5 collective-permute-start
  81.0 32.7 %collective-permute-done = bf16[2,96,4096]{2,1,0:T(8,128)(2,1)} collective-permute-done((bf16[2,96,4096]{2,1,0:T(8,128)(2,1)}, bf16[2,96,4096]{2,1,0:T(8,128)(2,1)}, u32[]{:S(2)}, u32[]{:S(2)}) %collective-permute-start) | collective-permute-done | bytes 1572896 | tf_op jit(solution)/shard_map/ppermute | solution.py:18
  124.4 45.4 %all-reduce.41.cloned.1.call-done = bf16[2,96,4096]{2,1,0:T(8,128)(2,1)} async-done(((bf16[2,96,4096]{2,1,0:T(8,128)(2,1)}), bf16[2,96,4096]{2,1,0:T(8,128)(2,1)}) %all-reduce.41.cloned.1.call-update) | async-done | bytes 1572880 | tf_op jit(solution)/shard_map/psum | solution.py:131
  176.2 33.3 %collective-permute-done.1 = bf16[2,96,4096]{2,1,0:T(8,128)(2,1)S(1)} collective-permute-done((bf16[2,96,4096]{2,1,0:T(8,128)(2,1)S(1)}, bf16[2,96,4096]{2,1,0:T(8,128)(2,1)S(1)}, u32[]{:S(2)}, u32[]{:S(2)}) %collective-permute-start.1) | collective-permute-done | bytes 1572896 | tf_op jit(solution)/shard_map/ppermute | solution.py:18
  220.2 44.0 %all-reduce.43.cloned.1.call-done = bf16[2,96,4096]{2,1,0:T(8,128)(2,1)} async-done(((bf16[2,96,4096]{2,1,0:T(8,128)(2,1)}), bf16[2,96,4096]{2,1,0:T(8,128)(2,1)}) %all-reduce.43.cloned.1.call-update) | async-done | bytes 1572880 | tf_op jit(solution)/shard_map/psum | solution.py:131
  273.3 31.3 %collective-permute-done.2 = bf16[2,96,4096]{2,1,0:T(8,128)(2,1)} collective-permute-done((bf16[2,96,4096]{2,1,0:T(8,128)(2,1)}, bf16[2,96,4096]{2,1,0:T(8,128)(2,1)}, u32[]{:S(2)}, u32[]{:S(2)}) %collective-permute-start.2) | collective-permute-done | bytes 1572896 | tf_op jit(solution)/shard_map/ppermute | solution.py:18
  326.7 41.8 %all-reduce.45.cloned.1.call-done = bf16[2,96,4096]{2,1,0:T(8,128)(2,1)} async-done(((bf16[2,96,4096]{2,1,0:T(8,128)(2,1)}), bf16[2,96,4096]{2,1,0:T(8,128)(2,1)}) %all-reduce.45.cloned.1.call-update) | async-done | bytes 1572880 | tf_op jit(solution)/shard_map/psum | solution.py:131
  373.0 4.6 all-gather.1
  402.4 43.0 %all-reduce.47.cloned.1.call-done = bf16[2,96,4096]{2,1,0:T(8,128)(2,1)} async-done(((bf16[2,96,4096]{2,1,0:T(8,128)(2,1)}), bf16[2,96,4096]{2,1,0:T(8,128)(2,1)}) %all-reduce.47.cloned.1.call-update) | async-done | bytes 1572880 | tf_op jit(solution)/shard_map/psum | solution.py:157
  451.2 36.2 %collective-permute-done.3 = bf16[2,96,4096]{2,1,0:T(8,128)(2,1)S(1)} collective-permute-done((bf16[2,96,4096]{2,1,0:T(8,128)(2,1)S(1)}, bf16[2,96,4096]{2,1,0:T(8,128)(2,1)S(1)}, u32[]{:S(2)}, u32[]{:S(2)}) %collective-permute-start.3) | collective-permute-done | bytes 1572896 | tf_op jit(solution)/shard_map/ppermute | solution.py:18
  503.0 42.1 %all-reduce.49.cloned.1.call-done = bf16[2,96,4096]{2,1,0:T(8,128)(2,1)} async-done(((bf16[2,96,4096]{2,1,0:T(8,128)(2,1)}), bf16[2,96,4096]{2,1,0:T(8,128)(2,1)}) %all-reduce.49.cloned.1.call-update) | async-done | bytes 1572880 | tf_op jit(solution)/shard_map/psum | solution.py:157
  550.4 36.4 %collective-permute-done.4 = bf16[2,96,4096]{2,1,0:T(8,128)(2,1)S(1)} collective-permute-done((bf16[2,96,4096]{2,1,0:T(8,128)(2,1)S(1)}, bf16[2,96,4096]{2,1,0:T(8,128)(2,1)S(1)}, u32[]{:S(2)}, u32[]{:S(2)}) %collective-permute-start.4) | collective-permute-done | bytes 1572896 | tf_op jit(solution)/shard_map/ppermute | solution.py:18
  602.5 42.2 %all-reduce.51.cloned.1.call-done = bf16[2,96,4096]{2,1,0:T(8,128)(2,1)} async-done(((bf16[2,96,4096]{2,1,0:T(8,128)(2,1)}), bf16[2,96,4096]{2,1,0:T(8,128)(2,1)}) %all-reduce.51.cloned.1.call-update) | async-done | bytes 1572880 | tf_op jit(solution)/shard_map/psum | solution.py:157
  661.1 4.6 all-to-all-start
  676.2 5.6 mul.2560
  682.4 9.3 %all_gather.11 = bf16[384,512]{1,0:T(8,128)(2,1)} all-gather(bf16[192,512]{1,0:T(8,128)(2,1)} %bitcast.1023), channel_id=1, replica_groups=mesh['section'=4,'dp'=2,'mp'=4] {'dp'}, dimensions={0}, use_global_device_ids=true | all-gather | bytes 589824 | tf_op jit(solution)/shard_map/all_gather | solution.py:241
  723.2 8.6 %all_gather.10 = bf16[384,768]{1,0:T(8,128)(2,1)S(1)} all-gather(bf16[192,768]{1,0:T(8,128)(2,1)S(1)} %maximum_select_fusion), channel_id=1, replica_groups=mesh['section'=4,'dp'=2,'mp'=4] {'dp'}, dimensions={0}, use_global_device_ids=true | all-gather | bytes 884736 | tf_op jit(solution)/shard_map/all_gather | solution.py:240
  731.8 5.4 fusion.63
  737.1 4.9 all-to-all-start.1
  752.7 24.6 %all-reduce.30 = f32[4096]{0:T(1024)S(1)} all-reduce(f32[4096]{0:T(1024)S(1)} %select_select_fusion), channel_id=3, replica_groups=mesh['section'=4,'dp'=2,'mp'=4] {'dp','mp'}, use_global_device_ids=true, to_apply=%region_90.91.clone | all-reduce | flops 4096 | bytes 32768
  777.9 4.7 slice_bitcast_fusion
  782.6 4.7 convolution_bitcast_fusion
  (496 shorter events, 210.8 us)
Async XLA Ops:
  7.2 66.2 %all-reduce.39.cloned.1.call-start = ((), (), s32[]{:S(2)}) async-start(), calls=%async_computation.2 | async-start | bytes 3145728 | tf_op jit(solution)/shard_map/psum | solution.py:131
  7.3 317.0 %copy-start.62 = (pred[96,96]{0,1:T(8,128)(4,1)}, pred[96,96]{0,1:T(8,128)(4,1)S(1)}, u32[]{:S(2)}) copy-start(pred[96,96]{0,1:T(8,128)(4,1)S(1)} %iota_compare_fusion) | copy-start | bytes 27652
  27.6 142.1 %all-reduce.41.cloned.1.call-start = ((), (), s32[]{:S(2)}) async-start(), calls=%async_computation.3 | async-start | bytes 3145728 | tf_op jit(solution)/shard_map/psum | solution.py:131
  76.5 37.2 %collective-permute-start = (bf16[2,96,4096]{2,1,0:T(8,128)(2,1)}, bf16[2,96,4096]{2,1,0:T(8,128)(2,1)}, u32[]{:S(2)}, u32[]{:S(2)}) collective-permute-start(bf16[2,96,4096]{2,1,0:T(8,128)(2,1)} %fusion.25), channel_id=1, source_target_pairs={{0,8},{8,16},{16,24},{1,9},{9,17},{17,25},{2,10},{10,18},{18,26},{... | collective-permute-start | bytes 4718600 | tf_op jit(solution)/shard_map/ppermute | solution.py:18
  124.3 140.0 %all-reduce.43.cloned.1.call-start = ((), (), s32[]{:S(2)}) async-start(), calls=%async_computation.4 | async-start | bytes 3145728 | tf_op jit(solution)/shard_map/psum | solution.py:131
  172.2 37.2 %collective-permute-start.1 = (bf16[2,96,4096]{2,1,0:T(8,128)(2,1)S(1)}, bf16[2,96,4096]{2,1,0:T(8,128)(2,1)S(1)}, u32[]{:S(2)}, u32[]{:S(2)}) collective-permute-start(bf16[2,96,4096]{2,1,0:T(8,128)(2,1)S(1)} %fusion.29), channel_id=1, source_target_pairs={{0,8},{8,16},{16,24},{1,9},{9,17},{17,25},{2,10},{10,18},{18,26},{... | collective-permute-start | bytes 4718600 | tf_op jit(solution)/shard_map/ppermute | solution.py:18
  215.7 48.6 %copy-start.24 = (bf16[2,96,4096]{2,1,0:T(8,128)(2,1)S(1)}, bf16[2,96,4096]{2,1,0:T(8,128)(2,1)}, u32[]{:S(2)}) copy-start(bf16[2,96,4096]{2,1,0:T(8,128)(2,1)} %copy-done.23) | copy-start | bytes 4718596
  220.2 51.8 %copy-start.114 = (s32[1,2]{1,0:T(1,128)S(1)}, s32[1,2]{1,0:T(1,128)}, u32[]{:S(2)}) copy-start(s32[1,2]{1,0:T(1,128)} %param.9) | copy-start | bytes 28
  220.2 148.3 %all-reduce.45.cloned.1.call-start = ((), (), s32[]{:S(2)}) async-start(), calls=%async_computation.5 | async-start | bytes 3145728 | tf_op jit(solution)/shard_map/psum | solution.py:131
  267.4 37.2 %collective-permute-start.2 = (bf16[2,96,4096]{2,1,0:T(8,128)(2,1)}, bf16[2,96,4096]{2,1,0:T(8,128)(2,1)}, u32[]{:S(2)}, u32[]{:S(2)}) collective-permute-start(bf16[2,96,4096]{2,1,0:T(8,128)(2,1)} %fusion.33), channel_id=1, source_target_pairs={{0,8},{8,16},{16,24},{1,9},{9,17},{17,25},{2,10},{10,18},{18,26},{... | collective-permute-start | bytes 4718600 | tf_op jit(solution)/shard_map/ppermute | solution.py:18
  323.9 121.5 %all-reduce.47.cloned.1.call-start = ((), (), s32[]{:S(2)}) async-start(), calls=%async_computation.6 | async-start | bytes 3145728 | tf_op jit(solution)/shard_map/psum | solution.py:157
  324.3 71.7 %copy-start.60 = (bf16[2,96,4,128]{3,1,2,0:T(8,128)(2,1)}, bf16[2,96,4,128]{3,1,2,0:T(8,128)(2,1)S(1)}, u32[]{:S(2)}) copy-start(bf16[2,96,4,128]{3,1,2,0:T(8,128)(2,1)S(1)} %pad_maximum_fusion) | copy-start | bytes 589828
  324.6 71.7 %copy-start.88 = (f32[2,4,96]{2,1,0:T(4,128)}, f32[2,4,96]{2,1,0:T(4,128)S(1)}, u32[]{:S(2)}) copy-start(f32[2,4,96]{2,1,0:T(4,128)S(1)} %get-tuple-element.178) | copy-start | bytes 9220
  324.7 71.6 %copy-start.103 = (f32[2,4,96]{2,1,0:T(4,128)}, f32[2,4,96]{2,1,0:T(4,128)S(1)}, u32[]{:S(2)}) copy-start(f32[2,4,96]{2,1,0:T(4,128)S(1)} %fusion.513) | copy-start | bytes 9220
  324.7 69.9 %copy-start.92 = (f32[2,4,96]{2,1,0:T(4,128)}, f32[2,4,96]{2,1,0:T(4,128)S(1)}, u32[]{:S(2)}) copy-start(f32[2,4,96]{2,1,0:T(4,128)S(1)} %multiply_divide_fusion) | copy-start | bytes 9220
  326.7 68.0 %copy-start.53 = (bf16[2,96,128,1]{2,1,3,0:T(8,128)(2,1)}, bf16[2,96,128,1]{2,1,3,0:T(8,128)(2,1)S(1)}, u32[]{:S(2)}) copy-start(bf16[2,96,128,1]{2,1,3,0:T(8,128)(2,1)S(1)} %fusion.144) | copy-start | bytes 147460
  402.4 142.8 %all-reduce.49.cloned.1.call-start = ((), (), s32[]{:S(2)}) async-start(), calls=%async_computation.7 | async-start | bytes 3145728 | tf_op jit(solution)/shard_map/psum | solution.py:157
  449.4 38.0 %collective-permute-start.3 = (bf16[2,96,4096]{2,1,0:T(8,128)(2,1)S(1)}, bf16[2,96,4096]{2,1,0:T(8,128)(2,1)S(1)}, u32[]{:S(2)}, u32[]{:S(2)}) collective-permute-start(bf16[2,96,4096]{2,1,0:T(8,128)(2,1)S(1)} %fusion.42), channel_id=1, source_target_pairs={{8,0},{16,8},{24,16},{9,1},{17,9},{25,17},{10,2},{18,10},{26,18},{... | collective-permute-start | bytes 4718600 | tf_op jit(solution)/shard_map/ppermute | solution.py:18
  503.0 141.7 %all-reduce.51.cloned.1.call-start = ((), (), s32[]{:S(2)}) async-start(), calls=%async_computation.8 | async-start | bytes 3145728 | tf_op jit(solution)/shard_map/psum | solution.py:157
  547.5 42.2 %copy-start.7 = (bf16[1,512,4096]{2,1,0:T(8,128)(2,1)S(1)}, bf16[1,512,4096]{2,1,0:T(8,128)(2,1)}, u32[]{:S(2)}) copy-start(bf16[1,512,4096]{2,1,0:T(8,128)(2,1)} %param.15) | copy-start | bytes 12582916
  548.9 37.9 %collective-permute-start.4 = (bf16[2,96,4096]{2,1,0:T(8,128)(2,1)S(1)}, bf16[2,96,4096]{2,1,0:T(8,128)(2,1)S(1)}, u32[]{:S(2)}, u32[]{:S(2)}) collective-permute-start(bf16[2,96,4096]{2,1,0:T(8,128)(2,1)S(1)} %fusion.39), channel_id=1, source_target_pairs={{8,0},{16,8},{24,16},{9,1},{17,9},{25,17},{10,2},{18,10},{26,18},{... | collective-permute-start | bytes 4718600 | tf_op jit(solution)/shard_map/ppermute | solution.py:18
  649.6 53.3 %collective-permute-start.5 = (bf16[2,96,4096]{2,1,0:T(8,128)(2,1)}, bf16[2,96,4096]{2,1,0:T(8,128)(2,1)}, u32[]{:S(2)}, u32[]{:S(2)}) collective-permute-start(bf16[2,96,4096]{2,1,0:T(8,128)(2,1)} %fusion.41), channel_id=1, source_target_pairs={{8,0},{16,8},{24,16},{9,1},{17,9},{25,17},{10,2},{18,10},{26,18},{... | collective-permute-start | bytes 4718600 | tf_op jit(solution)/shard_map/ppermute | solution.py:18
  661.1 76.0 %all-to-all-start = ((bf16[192,2,2048]{2,0,1:T(8,128)(2,1)}), bf16[192,2,2048]{2,0,1:T(8,128)(2,1)}, u32[]{:S(2)}, u32[]{:S(2)}) async-start(bf16[192,2,2048]{2,0,1:T(8,128)(2,1)} %copy.95), calls=%async_computation | async-start | bytes 3145728 | tf_op jit(solution)/shard_map/all_to_all | solution.py:237
  737.1 45.5 %all-to-all-start.1 = ((bf16[192,2,2048]{2,0,1:T(8,128)(2,1)}), bf16[192,2,2048]{2,0,1:T(8,128)(2,1)}, u32[]{:S(2)}, u32[]{:S(2)}) async-start(bf16[192,2,2048]{2,0,1:T(8,128)(2,1)} %fusion.63), calls=%async_computation.1 | async-start | bytes 3145728 | tf_op jit(solution)/shard_map/all_to_all | solution.py:238
  (106 other events, 641.8 us)
Sparse Core Ops, SparseCore 0:
  27.8 45.5 all-reduce.38
  124.4 45.3 all-reduce.40
  220.3 43.9 all-reduce.42
  324.1 44.3 all-reduce.44
  402.5 42.9 all-reduce.46
  503.1 41.9 all-reduce.48
  602.6 41.9 all-reduce.50
where the time goes:
time: 805 us; the launch traced here: 795 us
  waiting for transfers between devices  474 us (59%)
  matrix products  102 us (13%)
  local copies, waits for them, and re-layouts  66.7 us (8%)
  other arithmetic  55.3 us (7%)
  blocking collectives  47.1 us (6%)
  starting transfers between devices  27.3 us (3%)
  between operations  21.9 us (3%)
    psum x4, waiting for transfers between devices, forward_section(): lax.psum(partial_value.astype(jnp.bfloat16), 'mp').astype(jnp.float32)  177 us
    ppermute x6, waiting for transfers between devices, passed_along(): lax.ppermute(value, axis, [(source, source + steps) for source in range(f...  170 us
    psum x3, waiting for transfers between devices, backward_section(): lax.psum(member_grad.astype(jnp.bfloat16), 'mp').astype(jnp.float32)  127 us
    unnamed x1, blocking collectives  24.6 us
    dot_general x16, matrix products, contract_last(): lax.dot_general(left, right, (((left.ndim - 1,), (1,)), ((), ())), prefer...  24.5 us
    unnamed x237, local copies, waits for them, and re-layouts  18.1 us
    dot_general x13, matrix products, attend(): jnp.einsum('skgij,sjke->sikge', weights.astype(jnp.float32), values.astyp...  17.9 us
    ppermute x6, starting transfers between devices, passed_along(): lax.ppermute(value, axis, [(source, source + steps) for source in range(f...  17.6 us
  transfers between devices with their start and end apart: 15, of which 12 were waited for; matrix products, arithmetic and copies ran while one was open for 9% of the time, Pallas kernels for 0%

commit v1 on v0

v1 whole, which is shorter than its diff:
```python
import functools

import jax
import jax.numpy as jnp
from jax import lax
from jax.experimental import pallas as pl
from jax.experimental.pallas import tpu as pltpu
from jax.sharding import PartitionSpec as P

HEAD = 128
WIDTHS = 7


EPSILON = 1e-05
SOFTMAX_TEMPER = 0.05
ROPE_BASE = 500000.0


def rope_tables(length, head_size):
    half_size = head_size // 2
    inverse_freq = ROPE_BASE ** (-jnp.arange(half_size, dtype=jnp.float32) * 2.0 / head_size)
    angles = jnp.arange(length, dtype=jnp.float32)[:, None] * inverse_freq[None, :]
    return (jnp.cos(angles), jnp.sin(angles))


def rotate(values, cosine, sine_table):
    half_size = values.shape[-1] // 2
    first_half = values[..., :half_size]
    second = values[..., half_size:]
    cosine = cosine[None, :, None, :]
    sine_table = sine_table[None, :, None, :]
    return jnp.concatenate(
        [first_half * cosine - second * sine_table, second * cosine + first_half * sine_table],
        axis=-1,
    )


def attend(query_pre, key_pre, value_pre):
    seq_count, length, query_width = query_pre.shape
    query_heads = query_width // HEAD
    kv_heads = key_pre.shape[-1] // HEAD
    group_size = query_heads // kv_heads
    cosine, sine_table = rope_tables(length, HEAD)
    query_vectors = rotate(
        query_pre.reshape(seq_count, length, query_heads, HEAD), cosine, sine_table
    ).astype(jnp.bfloat16)
    key_rows = rotate(
        key_pre.reshape(seq_count, length, kv_heads, HEAD), cosine, sine_table
    ).astype(jnp.bfloat16)
    values = value_pre.reshape(seq_count, length, kv_heads, HEAD).astype(jnp.bfloat16)
    query_vectors = query_vectors.reshape(seq_count, length, kv_heads, group_size, HEAD)
    scores = jnp.einsum(
        "sikge,sjke->skgij", query_vectors.astype(jnp.float32), key_rows.astype(jnp.float32)
    ) * HEAD ** (-0.5)
    causal = (
        jnp.arange(length, dtype=jnp.int32)[:, None] >= jnp.arange(length, dtype=jnp.int32)[None, :]
    )
    scores = jnp.where(causal, scores, -1e30)
    weights = jax.nn.softmax(scores, axis=-1).astype(jnp.bfloat16)
    mixture = jnp.einsum(
        "skgij,sjke->sikge", weights.astype(jnp.float32), values.astype(jnp.float32)
    )
    return mixture.reshape(seq_count, length, query_heads * HEAD)


def normalize(hidden_f, gain_vector):
    inv_rms = lax.rsqrt(jnp.mean(hidden_f * hidden_f, axis=-1, keepdims=True) + EPSILON)
    return hidden_f * inv_rms * gain_vector


def contract_rows(left, right):
    return lax.dot_general(
        left, right, (((0,), (0,)), ((), ())), preferred_element_type=jnp.float32
    )


def contract_last(left, right):
    return lax.dot_general(
        left, right, (((left.ndim - 1,), (1,)), ((), ())), preferred_element_type=jnp.float32
    )


def spread_grad(exit_grad, mask_of_valid, counts):
    return mask_of_valid[:, :, None] * (exit_grad / counts[:, None])[:, None, :]


def matryoshka_losses(pooled, positives):
    pair_total = pooled.shape[0]
    target = (jnp.arange(pair_total, dtype=jnp.int32)[None, :] == positives[:, None]).astype(
        jnp.float32
    )
    losses = []
    for level_index in range(WIDTHS):
        leading_width = pooled.shape[-1] // 2**level_index
        query_vectors = pooled[:, 0, :leading_width]
        passage_rows = pooled[:, 1, :leading_width]
        query_vectors = query_vectors * lax.rsqrt(
            jnp.mean(query_vectors * query_vectors, axis=-1, keepdims=True) + 1e-06
        )
        passage_rows = passage_rows * lax.rsqrt(
            jnp.mean(passage_rows * passage_rows, axis=-1, keepdims=True) + 1e-06
        )
        score_matrix = jnp.dot(query_vectors, passage_rows.T, precision=lax.Precision.HIGHEST) / (
            leading_width * SOFTMAX_TEMPER
        )
        picked = jnp.sum(score_matrix * target, axis=-1)
        losses.append(jnp.mean(jax.nn.logsumexp(score_matrix, axis=-1) - picked))
    return jnp.stack(losses)


MESH = pl.DeviceIdType.MESH
ROW_TILE = 16


def mp_place(me, levels):
    bits = [(me // (1 << level)) % 2 for level in range(levels)]
    partners = [me + (1 - 2 * bits[level]) * (1 << level) for level in range(levels)]
    return bits, partners


def shard_offset(bits, rows, flips=0):
    offset = 0
    for level, bit in enumerate(bits):
        bit = 1 - bit if (flips >> level) & 1 else bit
        offset = offset + bit * (rows >> (level + 1))
    return offset


def rows_at(start, size):
    return pl.ds(pl.multiple_of(start, ROW_TILE), size)


def scatter_kernel(levels, part_ref, out_ref, *scratch):
    arrived, kept = scratch[:levels], scratch[levels : 2 * levels - 1]
    send_sem, recv_sem = scratch[2 * levels - 1 :]
    bits, partners = mp_place(lax.axis_index("mp"), levels)
    barrier = pltpu.get_barrier_semaphore()
    for partner in partners:
        pl.semaphore_signal(barrier, inc=1, device_id={"mp": partner}, device_id_type=MESH)
    pl.semaphore_wait(barrier, levels)
    held = part_ref
    for level in range(levels):
        half = held.shape[0] // 2
        copy = pltpu.make_async_remote_copy(
            src_ref=held.at[rows_at((1 - bits[level]) * half, half)],
            dst_ref=arrived[level],
            send_sem=send_sem.at[level],
            recv_sem=recv_sem.at[level],
            device_id={"mp": partners[level]},
            device_id_type=MESH,
        )
        copy.start()
        copy.wait()
        target = out_ref if level == levels - 1 else kept[level]

        def add(step, carry, held=held, half=half, target=target, level=level):
            own = held[rows_at(bits[level] * half + step * ROW_TILE, ROW_TILE), :]
            other = arrived[level][rows_at(step * ROW_TILE, ROW_TILE), :]
            total = own.astype(jnp.float32) + other.astype(jnp.float32)
            target[rows_at(step * ROW_TILE, ROW_TILE), :] = total.astype(target.dtype)
            return carry

        lax.fori_loop(0, half // ROW_TILE, add, 0)
        held = target


def scatter_rows(partial_value):
    rows, width = partial_value.shape
    members = lax.axis_size("mp")
    levels = members.bit_length() - 1
    arrived = [pltpu.VMEM((rows >> (level + 1), width), jnp.bfloat16) for level in range(levels)]
    return pl.pallas_call(
        functools.partial(scatter_kernel, levels),
        out_shape=jax.ShapeDtypeStruct((rows // members, width), jnp.float32),
        in_specs=[pl.BlockSpec(memory_space=pltpu.VMEM)],
        out_specs=pl.BlockSpec(memory_space=pltpu.VMEM),
        scratch_shapes=arrived
        + arrived[:-1]
        + [pltpu.SemaphoreType.DMA((levels,)), pltpu.SemaphoreType.DMA((levels,))],
        compiler_params=pltpu.CompilerParams(collective_id=0, has_side_effects=True),
        name="scatter_rows",
    )(partial_value)


def relay_kernel(levels, direction, shard_ref, out_ref, relay_send, relay_recv, send_sem, recv_sem):
    members = 1 << levels
    shard_rows = shard_ref.shape[0]
    rows = out_ref.shape[0]
    chunks = shard_rows // ROW_TILE
    here = lax.axis_index("section")
    count = lax.axis_size("section")
    if direction > 0:
        has_source, has_target = here > 0, here < count - 1
    else:
        has_source, has_target = here < count - 1, here > 0
    bits, partners = mp_place(lax.axis_index("mp"), levels)
    barrier = pltpu.get_barrier_semaphore()

    @pl.when(has_source)
    def _():
        pl.semaphore_signal(
            barrier, inc=1, device_id={"section": here - direction}, device_id_type=MESH
        )
        for partner in partners:
            pl.semaphore_signal(barrier, inc=1, device_id={"mp": partner}, device_id_type=MESH)

    @pl.when(jnp.logical_and(has_source, has_target))
    def _():
        pl.semaphore_wait(barrier, levels + 1)

    @pl.when(jnp.logical_and(has_source, jnp.logical_not(has_target)))
    def _():
        pl.semaphore_wait(barrier, levels)

    @pl.when(jnp.logical_and(has_target, jnp.logical_not(has_source)))
    def _():
        pl.semaphore_wait(barrier, 1)

    def piece(chunk, flips):
        return out_ref.at[rows_at(shard_offset(bits, rows, flips) + chunk * ROW_TILE, ROW_TILE)]

    def relay(chunk):
        return pltpu.make_async_remote_copy(
            src_ref=shard_ref.at[pl.ds(chunk * ROW_TILE, ROW_TILE)],
            dst_ref=piece(chunk, 0),
            send_sem=relay_send.at[chunk],
            recv_sem=relay_recv.at[chunk],
            device_id={"section": here + direction},
            device_id_type=MESH,
        )

    def spread(chunk, flips, level):
        slot = (flips | (1 << level)) - 1
        return pltpu.make_async_remote_copy(
            src_ref=piece(chunk, flips),
            dst_ref=piece(chunk, flips),
            send_sem=send_sem.at[chunk, slot],
            recv_sem=recv_sem.at[chunk, slot],
            device_id={"mp": partners[level]},
            device_id_type=MESH,
        )

    def incoming(chunk, flips):
        level = (flips & -flips).bit_length() - 1
        return pltpu.make_async_remote_copy(
            src_ref=piece(chunk, flips),
            dst_ref=piece(chunk, flips),
            send_sem=send_sem.at[chunk, flips - 1],
            recv_sem=recv_sem.at[chunk, flips - 1],
            device_id={"mp": partners[level]},
            device_id_type=MESH,
        )

    @pl.when(has_target)
    def _():
        for chunk in range(chunks):
            relay(chunk).start()

    @pl.when(has_source)
    def _():
        sent = []
        order = sorted(range(1, members), key=lambda flips: -(flips & -flips))
        for chunk in range(chunks):
            relay(chunk).wait_recv()
            for level in reversed(range(levels)):
                copy = spread(chunk, 0, level)
                copy.start()
                sent.append(copy)
        for chunk in range(chunks):
            for flips in order:
                incoming(chunk, flips).wait_recv()
                lowest = (flips & -flips).bit_length() - 1
                for level in reversed(range(lowest)):
                    copy = spread(chunk, flips, level)
                    copy.start()
                    sent.append(copy)
        for copy in sent:
            copy.wait_send()

    @pl.when(jnp.logical_not(has_source))
    def _():
        def clear(step, carry):
            out_ref[rows_at(step * ROW_TILE, ROW_TILE), :] = jnp.zeros(
                (ROW_TILE, out_ref.shape[1]), out_ref.dtype
            )
            return carry

        lax.fori_loop(0, rows // ROW_TILE, clear, 0)

    @pl.when(has_target)
    def _():
        for chunk in range(chunks):
            relay(chunk).wait_send()


def relay_rows(shard, direction):
    shard_rows, width = shard.shape
    members = lax.axis_size("mp")
    levels = members.bit_length() - 1
    chunks = shard_rows // ROW_TILE
    return pl.pallas_call(
        functools.partial(relay_kernel, levels, direction),
        out_shape=jax.ShapeDtypeStruct((shard_rows * members, width), jnp.bfloat16),
        in_specs=[pl.BlockSpec(memory_space=pltpu.VMEM)],
        out_specs=pl.BlockSpec(memory_space=pltpu.VMEM),
        scratch_shapes=[
            pltpu.SemaphoreType.DMA((chunks,)),
            pltpu.SemaphoreType.DMA((chunks,)),
            pltpu.SemaphoreType.DMA((chunks, members - 1)),
            pltpu.SemaphoreType.DMA((chunks, members - 1)),
        ],
        compiler_params=pltpu.CompilerParams(
            collective_id=1 if direction > 0 else 2, has_side_effects=True
        ),
        name="relay_forward" if direction > 0 else "relay_backward",
    )(shard)


def local(entrance, lengths, positives, norm_gains, query_proj, key_proj, value_proj, out_proj):
    section_count = lax.axis_size("section")
    section_index = lax.axis_index("section")
    member_count = lax.axis_size("mp")
    dp_count = lax.axis_size("dp")
    pair_count = entrance.shape[0]
    seq_count = 2 * pair_count
    length = entrance.shape[2]
    width_all = entrance.shape[3]
    rows = seq_count * length
    shard_rows = rows // member_count
    bits, _ = mp_place(lax.axis_index("mp"), member_count.bit_length() - 1)
    offset = shard_offset(bits, rows)
    start_hidden = entrance.reshape(rows, width_all)
    mask_of_valid = (
        jnp.arange(length, dtype=jnp.int32)[None, :] < lengths.reshape(seq_count, 1)
    ).astype(jnp.float32)
    counts = jnp.sum(mask_of_valid, axis=1)
    gain_vector = norm_gains[0]
    head_weight = jnp.concatenate([query_proj[0], key_proj[0], value_proj[0]], axis=1)
    out_weight = out_proj[0]
    query_cols = query_proj.shape[2]
    kv_cols = key_proj.shape[2]

    def own_rows(values):
        return lax.dynamic_slice_in_dim(values, offset, shard_rows, 0)

    def attend_heads(heads):
        heads = heads.reshape(seq_count, length, -1)
        mixed = attend(
            heads[..., :query_cols],
            heads[..., query_cols : query_cols + kv_cols],
            heads[..., query_cols + kv_cols :],
        )
        return mixed.reshape(rows, -1)

    current = start_hidden
    for section_turn in range(section_count):
        normed = normalize(current.astype(jnp.float32), gain_vector).astype(jnp.bfloat16)
        heads = jnp.dot(normed, head_weight, preferred_element_type=jnp.float32)
        if section_turn + 1 == section_count:
            break
        mixture = attend_heads(heads).astype(jnp.bfloat16)
        partial_value = jnp.dot(mixture, out_weight, preferred_element_type=jnp.float32)
        total_value = scatter_rows(partial_value.astype(jnp.bfloat16))
        produced = own_rows(current).astype(jnp.float32) + total_value
        arrived = relay_rows(produced.astype(jnp.bfloat16), 1)
        current = jnp.where(section_index == 0, start_hidden, arrived)
    mixture_f, attend_pull = jax.vjp(attend_heads, heads)
    mixture = mixture_f.astype(jnp.bfloat16)
    hidden_f = current.astype(jnp.float32)
    inv_rms = lax.rsqrt(jnp.mean(hidden_f * hidden_f, axis=-1, keepdims=True) + EPSILON)

    token_mask = mask_of_valid[:, :, None]
    mixture_sum = jnp.sum(
        mixture.astype(jnp.float32).reshape(seq_count, length, -1) * token_mask, axis=1
    )
    coarse = mixture_sum.astype(jnp.bfloat16)
    fine = (mixture_sum - coarse.astype(jnp.float32)).astype(jnp.bfloat16)
    both = jnp.dot(
        jnp.concatenate([coarse, fine], axis=0), out_weight, preferred_element_type=jnp.float32
    )
    hidden_sum = jnp.sum(hidden_f.reshape(seq_count, length, -1) * token_mask, axis=1)
    pooled = both[:seq_count] + both[seq_count:]
    pooled = pooled + jnp.where(lax.axis_index("mp") == 0, hidden_sum, 0.0)
    pooled = pooled / counts[:, None]
    gathered = lax.all_gather(pooled, ("dp", "mp"), axis=0)
    gathered = jnp.sum(gathered.reshape(dp_count, member_count, seq_count, width_all), axis=1)
    gathered = gathered.reshape(dp_count * pair_count, 2, width_all)
    losses_now, pullback = jax.vjp(
        lambda embedded: matryoshka_losses(embedded, positives), gathered
    )
    pair_grads = pullback(jnp.ones((WIDTHS,), jnp.float32))[0]
    own_grad = lax.dynamic_slice_in_dim(
        pair_grads, lax.axis_index("dp") * pair_count, pair_count, 0
    )
    token_grad = spread_grad(own_grad.reshape(seq_count, width_all), mask_of_valid, counts)
    token_grad = token_grad.reshape(rows, width_all)

    normed_cols = lax.all_to_all(normed, "dp", split_axis=1, concat_axis=0, tiled=True)
    mixture_piece = lax.all_gather(mixture, "dp", axis=0, tiled=True)
    shard_hidden = own_rows(current).astype(jnp.float32)
    _, norm_pull = jax.vjp(lambda values: normalize(values, gain_vector), shard_hidden)
    upstream = token_grad
    for section_turn in range(section_count):
        out_grad = upstream.astype(jnp.bfloat16)
        mixture_grad = contract_last(out_grad, out_weight).astype(jnp.bfloat16)
        pulled = attend_pull(lax.optimization_barrier(mixture_grad).astype(jnp.float32))[0]
        head_grads = pulled.astype(jnp.bfloat16)
        member_grad = contract_last(head_grads, head_weight).astype(jnp.bfloat16)
        if section_turn + 1 == section_count:
            break
        normed_grad = scatter_rows(member_grad)
        input_grad = (own_rows(upstream) + norm_pull(normed_grad)[0]).astype(jnp.bfloat16)
        arrived = relay_rows(input_grad, -1).astype(jnp.float32)
        upstream = token_grad + jnp.where(section_index == section_count - 1, 0.0, arrived)
    out_cols = lax.all_to_all(out_grad, "dp", split_axis=1, concat_axis=0, tiled=True)
    head_piece = lax.all_gather(head_grads, "dp", axis=0, tiled=True)
    gain_term = jnp.sum(member_grad.astype(jnp.float32) * hidden_f * inv_rms, axis=0)
    gain_parts = lax.all_to_all(
        gain_term.reshape(dp_count * member_count, -1),
        ("dp", "mp"),
        split_axis=0,
        concat_axis=0,
        tiled=True,
    )
    gain_share = jnp.sum(gain_parts, axis=0)
    return (
        losses_now[None],
        gain_share[None],
        contract_rows(normed_cols, head_piece[:, :query_cols])[None],
        contract_rows(normed_cols, head_piece[:, query_cols : query_cols + kv_cols])[None],
        contract_rows(normed_cols, head_piece[:, query_cols + kv_cols :])[None],
        contract_rows(mixture_piece, out_cols)[None],
    )


def solution(mesh):
    in_specs = (
        P("dp", None, None, None),
        P("dp", None),
        P(),
        P("section", None),
        P("section", None, "mp"),
        P("section", None, "mp"),
        P("section", None, "mp"),
        P("section", "mp", None),
    )
    out_specs = (
        P("section", None),
        P("section", ("dp", "mp")),
        P("section", "dp", "mp"),
        P("section", "dp", "mp"),
        P("section", "dp", "mp"),
        P("section", "mp", "dp"),
    )
    return jax.shard_map(local, mesh=mesh, in_specs=in_specs, out_specs=out_specs, check_vma=False)
```

time: 805 us -> 464 us (0.58)
  waiting for transfers between devices: 474 us -> 21.6 us
  Pallas kernels: 0 us -> 218 us
  local copies, waits for them, and re-layouts: 66.7 us -> 38.2 us
  matrix products: 102 us -> 75.2 us
  starting transfers between devices: 27.3 us -> 10.7 us
  between operations: 21.9 us -> 6.69 us
  other arithmetic: 55.3 us -> 44.6 us
    psum x7 -> x0, waiting for transfers between devices: 304 us -> none  [the longest x4 177 us: forward_section(): lax.psum(partial_value.astype(jnp.bfloat16), 'mp').astype(jnp.float32)]
    pallas_call x0 -> x12, Pallas kernels: none -> 218 us  [the longest x6 120 us: relay_rows(): pl.pallas_call(functools.partial(relay_kernel, levels, direction), out_sh...]
    ppermute x6 -> x0, waiting for transfers between devices: 170 us -> none  [passed_along(): lax.ppermute(value, axis, [(source, source + steps) for source in range(f...]
    unnamed x1 -> x0, blocking collectives: 24.6 us -> none
    all_to_all x2 -> x3, waiting for transfers between devices: 0.01 us -> 21.6 us  [the longest x1 18.2 us: local(): lax.all_to_all(normed, 'dp', split_axis=1, concat_axis=0, tiled=True)]
    dot_general x16 -> x8, matrix products: 38.4 us -> 19.5 us  [the longest x4 10.2 us: local(): heads = jnp.dot(normed, head_weight, preferred_element_type=jnp.float32)]
    ppermute x6 -> x0, starting transfers between devices: 17.6 us -> none  [passed_along(): lax.ppermute(value, axis, [(source, source + steps) for source in range(f...]
    all_gather x1, blocking collectives: 8.57 us -> 25 us  [local(): head_piece = lax.all_gather(head_grads, 'dp', axis=0, tiled=True)]
  transfers between devices with their start and end apart: 15 -> 3, of which waited for: 12 -> 2; matrix products, arithmetic and copies ran while one was open for 9% -> 3% of each run, Pallas kernels for 0% -> 0%
where the time goes in v1:
time: 464 us; the launch traced here: 456 us
  Pallas kernels  218 us (47%)
  matrix products  75.2 us (16%)
  other arithmetic  44.6 us (10%)
  blocking collectives  41.4 us (9%)
  local copies, waits for them, and re-layouts  38.2 us (8%)
  waiting for transfers between devices  21.6 us (5%)
  starting transfers between devices  10.7 us (2%)
  between operations  6.69 us (1%)
    pallas_call x6, Pallas kernels, relay_rows(): pl.pallas_call(functools.partial(relay_kernel, levels, direction), out_sh...  120 us
    pallas_call x6, Pallas kernels, scatter_rows(): pl.pallas_call(functools.partial(scatter_kernel, levels), out_shape=jax.S...  98.3 us
    dot_general x8, matrix products, contract_last(): lax.dot_general(left, right, (((left.ndim - 1,), (1,)), ((), ())), prefer...  27.7 us
    all_gather x1, blocking collectives, local(): head_piece = lax.all_gather(head_grads, 'dp', axis=0, tiled=True)  25 us
    unnamed x82, local copies, waits for them, and re-layouts  20.3 us
    all_to_all x1, waiting for transfers between devices, local(): lax.all_to_all(normed, 'dp', split_axis=1, concat_axis=0, tiled=True)  18.2 us
    dot_general x4, matrix products, contract_rows(): lax.dot_general(left, right, (((0,), (0,)), ((), ())), preferred_element_...  11.6 us
    dot_general x4, matrix products, local(): heads = jnp.dot(normed, head_weight, preferred_element_type=jnp.float32)  10.2 us
  transfers between devices with their start and end apart: 3, of which 2 were waited for; matrix products, arithmetic and copies ran while one was open for 3% of the time, Pallas kernels for 0%

profile of v1, /device:TPU:0, one launch (start us, length us, event | category | flops | bytes accessed | tf_op | source)
XLA Modules:
  0.0 456.1 jit_solution(2378800908264542953)
XLA Ops:
  4.1 4.8 %fusion = f32[2,96,768]{2,1,0:T(8,128)S(1)} fusion(bf16[1,2,96,4096]{3,2,1,0:T(8,128)(2,1)} %param.8, f32[4096]{0:T(1024)} %bitcast.819, f32[2,96]{1,0:T(2,128)S(1)} %add_rsqrt_fusion.3, bf16[4096,128]{1,0:T(8,128)(2,1)} %bitcast.877, bf16[4096,128]{1,0:T(8,128)(2,1)} %bitcast.885, bf16[4096,512]{1,0:T(8,128)(2,1)} %bitcast.869), kind=kOutput, calls=%fused_computation.1 | convolution fusion | flops 1229979648 | bytes 8471296 | tf_op jit(solution)/shard_map/dot_general | solution.py:358
  13.6 17.3 %scatter_rows.6 = f32[48,4096]{1,0:T(8,128)} custom-call(bf16[192,4096]{1,0:T(8,128)(2,1)} %convolution_convert_fusion.6.part_ref), custom_call_target="tpu_custom_call" | custom-call | tf_op jit(solution)/shard_map/scatter_rows/pallas_call | solution.py:172
  32.9 12.6 %relay_forward.3 = bf16[192,4096]{1,0:T(8,128)(2,1)} custom-call(bf16[48,4096]{1,0:T(8,128)(2,1)} %add_convert_fusion.2.shard_ref), custom_call_target="tpu_custom_call" | custom-call | tf_op jit(solution)/shard_map/relay_forward/pallas_call | solution.py:301
  59.8 16.2 %scatter_rows.7 = f32[48,4096]{1,0:T(8,128)} custom-call(bf16[192,4096]{1,0:T(8,128)(2,1)} %convolution_convert_fusion.5.part_ref), custom_call_target="tpu_custom_call" | custom-call | tf_op jit(solution)/shard_map/scatter_rows/pallas_call | solution.py:172
  78.0 20.2 %relay_forward.4 = bf16[192,4096]{1,0:T(8,128)(2,1)} custom-call(bf16[48,4096]{1,0:T(8,128)(2,1)} %add_convert_fusion.1.shard_ref), custom_call_target="tpu_custom_call" | custom-call | tf_op jit(solution)/shard_map/relay_forward/pallas_call | solution.py:301
  111.5 16.2 %scatter_rows.8 = f32[48,4096]{1,0:T(8,128)} custom-call(bf16[192,4096]{1,0:T(8,128)(2,1)} %convolution_convert_fusion.4.part_ref), custom_call_target="tpu_custom_call" | custom-call | tf_op jit(solution)/shard_map/scatter_rows/pallas_call | solution.py:172
  129.7 19.4 %relay_forward.5 = bf16[192,4096]{1,0:T(8,128)(2,1)} custom-call(bf16[48,4096]{1,0:T(8,128)(2,1)} %add_convert_fusion.shard_ref), custom_call_target="tpu_custom_call" | custom-call | tf_op jit(solution)/shard_map/relay_forward/pallas_call | solution.py:301
  159.3 9.8 %all-gather.1 = f32[8,2,4096]{2,1,0:T(2,128)S(1)} all-gather(f32[1,2,4096]{2,1,0:T(2,128)S(1)} %fusion.219), channel_id=2, replica_groups=mesh['section'=4,'dp'=2,'mp'=4] {'dp','mp'}, dimensions={0}, use_global_device_ids=true | all-gather | bytes 294912 | tf_op jit(solution)/shard_map/all_gather | solution.py:385
  187.7 4.5 fusion.50
  196.6 4.9 %convolution_convert_fusion.3.part_ref = bf16[192,4096]{1,0:T(8,128)(2,1)} fusion(bf16[192,768]{1,0:T(8,128)(2,1)S(1)} %bitcast.841, bf16[4096,128]{1,0:T(8,128)(2,1)} %bitcast.878, bf16[4096,128]{1,0:T(8,128)(2,1)} %bitcast.887, bf16[4096,512]{1,0:T(8,128)(2,1)S(1)} %bitcast.873), kind=kOutput, calls=%fused_computation.9 | convolution fusion | flops 1227620352 | bytes 8159232 | tf_op jit(solution)/shard_map/dot_general | solution.py:78
  201.4 16.2 %scatter_rows.9 = f32[48,4096]{1,0:T(8,128)} custom-call(bf16[192,4096]{1,0:T(8,128)(2,1)} %convolution_convert_fusion.3.part_ref), custom_call_target="tpu_custom_call" | custom-call | tf_op jit(solution)/shard_map/scatter_rows/pallas_call | solution.py:172
  220.5 28.4 %relay_backward.3 = bf16[192,4096]{1,0:T(8,128)(2,1)} custom-call(bf16[48,4096]{1,0:T(8,128)(2,1)} %fusion.102.shard_ref), custom_call_target="tpu_custom_call" | custom-call | tf_op jit(solution)/shard_map/relay_backward/pallas_call | solution.py:301
  262.8 16.2 %scatter_rows.10 = f32[48,4096]{1,0:T(8,128)} custom-call(bf16[192,4096]{1,0:T(8,128)(2,1)} %convolution_convert_fusion.2.part_ref), custom_call_target="tpu_custom_call" | custom-call | tf_op jit(solution)/shard_map/scatter_rows/pallas_call | solution.py:172
  282.7 19.7 %relay_backward.4 = bf16[192,4096]{1,0:T(8,128)(2,1)} custom-call(bf16[48,4096]{1,0:T(8,128)(2,1)} %fusion.104.shard_ref), custom_call_target="tpu_custom_call" | custom-call | tf_op jit(solution)/shard_map/relay_backward/pallas_call | solution.py:301
  316.3 16.2 %scatter_rows.11 = f32[48,4096]{1,0:T(8,128)} custom-call(bf16[192,4096]{1,0:T(8,128)(2,1)} %convolution_convert_fusion.1.part_ref), custom_call_target="tpu_custom_call" | custom-call | tf_op jit(solution)/shard_map/scatter_rows/pallas_call | solution.py:172
  336.2 19.2 %relay_backward.5 = bf16[192,4096]{1,0:T(8,128)(2,1)} custom-call(bf16[48,4096]{1,0:T(8,128)(2,1)} %fusion.106.shard_ref), custom_call_target="tpu_custom_call" | custom-call | tf_op jit(solution)/shard_map/relay_backward/pallas_call | solution.py:301
  358.6 4.5 fusion.63
  370.7 3.3 all-to-all-start
  375.3 3.4 all-to-all-done
  378.7 3.7 all-to-all-start.1
  383.6 18.2 %all-to-all-done.1 = bf16[192,2,2048]{2,0,1:T(8,128)(2,1)S(1)} async-done(((bf16[192,2,2048]{2,0,1:T(8,128)(2,1)}), bf16[192,2,2048]{2,0,1:T(8,128)(2,1)S(1)}, u32[]{:S(2)}, u32[]{:S(2)}) %all-to-all-start.1) | async-done | bytes 1572896 | tf_op jit(solution)/shard_map/all_to_all | solution.py:398
  401.8 3.7 all-to-all-start.2
  405.5 25.0 %all_gather.14 = bf16[384,768]{1,0:T(8,128)(2,1)} all-gather(bf16[192,768]{1,0:T(8,128)(2,1)S(1)} %bitcast.818), channel_id=1, replica_groups=mesh['section'=4,'dp'=2,'mp'=4] {'dp'}, dimensions={0}, use_global_device_ids=true | all-gather | bytes 884736 | tf_op jit(solution)/shard_map/all_gather | solution.py:416
  437.1 6.5 %all_gather.15 = bf16[384,512]{1,0:T(8,128)(2,1)S(1)} all-gather(bf16[192,512]{1,0:T(8,128)(2,1)} %bitcast.834), channel_id=1, replica_groups=mesh['section'=4,'dp'=2,'mp'=4] {'dp'}, dimensions={0}, use_global_device_ids=true | all-gather | bytes 589824 | tf_op jit(solution)/shard_map/all_gather | solution.py:399
  (326 shorter events, 139.4 us)
Async XLA Ops:
  11.5 19.5 %copy-start.5 = (bf16[1,2,96,4096]{3,2,1,0:T(8,128)(2,1)S(1)}, bf16[1,2,96,4096]{3,2,1,0:T(8,128)(2,1)}, u32[]{:S(2)}) copy-start(bf16[1,2,96,4096]{3,2,1,0:T(8,128)(2,1)} %param.8) | copy-start | bytes 4718596
  45.6 2.5 copy-start.29
  54.3 3.4 copy-start.1
  98.2 2.5 copy-start.30
  98.2 2.8 copy-start.35
  106.0 3.4 copy-start.2
  149.4 2.6 copy-start.24
  154.9 38.3 %copy-start.15 = (bf16[2,1,4,96,96]{3,4,2,0,1:T(8,128)(2,1)}, bf16[2,1,4,96,96]{3,4,2,0,1:T(8,128)(2,1)S(1)}, u32[]{:S(2)}) copy-start(bf16[2,1,4,96,96]{3,4,2,0,1:T(8,128)(2,1)S(1)} %divide_convert_fusion) | copy-start | bytes 442372
  156.3 16.5 %copy-start.19 = (s32[2]{0:T(128)S(1)}, s32[2]{0:T(128)}, u32[]{:S(2)}) copy-start(s32[2]{0:T(128)} %param.10) | copy-start | bytes 28
  170.9 9.8 %copy-start.20 = (f32[2]{0:T(128)}, f32[2]{0:T(128)S(1)}, u32[]{:S(2)}) copy-start(f32[2]{0:T(128)S(1)} %fusion.369) | copy-start | bytes 28
  170.9 9.0 %copy-start.21 = (f32[2]{0:T(128)}, f32[2]{0:T(128)S(1)}, u32[]{:S(2)}) copy-start(f32[2]{0:T(128)S(1)} %fusion.368) | copy-start | bytes 28
  248.9 3.7 copy-start.3
  252.7 3.2 copy-start.16
  256.7 2.5 copy-start.32
  256.8 2.8 copy-start.37
  302.4 3.7 copy-start.4
  310.3 2.8 copy-start.38
  364.9 2.8 copy-start.39
  367.7 6.4 %copy-start.10 = (bf16[192,4096]{1,0:T(8,128)(2,1)S(1)}, bf16[192,4096]{1,0:T(8,128)(2,1)}, u32[]{:S(2)}) copy-start(bf16[192,4096]{1,0:T(8,128)(2,1)} %copy-done.9) | copy-start | bytes 4718596
  370.7 8.0 %all-to-all-start = ((f32[8,1,512]{2,1,0:T(1,128)}), f32[8,1,512]{2,1,0:T(1,128)S(1)}, u32[]{:S(2)}, u32[]{:S(2)}) async-start(f32[8,1,512]{2,1,0:T(1,128)} %bitcast.193), calls=%async_computation | async-start | bytes 32768 | tf_op jit(solution)/shard_map/all_to_all | solution.py:418
  375.3 7.1 %copy-start.12 = (bf16[192,4096]{1,0:T(8,128)(2,1)S(1)}, bf16[192,4096]{1,0:T(8,128)(2,1)}, u32[]{:S(2)}) copy-start(bf16[192,4096]{1,0:T(8,128)(2,1)} %copy-done.11) | copy-start | bytes 4718596
  378.7 23.1 %all-to-all-start.1 = ((bf16[192,2,2048]{2,0,1:T(8,128)(2,1)}), bf16[192,2,2048]{2,0,1:T(8,128)(2,1)S(1)}, u32[]{:S(2)}, u32[]{:S(2)}) async-start(bf16[192,2,2048]{2,0,1:T(8,128)(2,1)} %bitcast.807), calls=%async_computation.1 | async-start | bytes 3145728 | tf_op jit(solution)/shard_map/all_to_all | solution.py:398
  401.8 50.8 %all-to-all-start.2 = ((bf16[192,2,2048]{2,0,1:T(8,128)(2,1)}), bf16[192,2,2048]{2,0,1:T(8,128)(2,1)S(1)}, u32[]{:S(2)}, u32[]{:S(2)}) async-start(bf16[192,2,2048]{2,0,1:T(8,128)(2,1)} %bitcast.806), calls=%async_computation.2 | async-start | bytes 3145728 | tf_op jit(solution)/shard_map/all_to_all | solution.py:415
  444.2 5.0 %copy-start.13 = (bf16[384,768]{1,0:T(8,128)(2,1)S(1)}, bf16[384,768]{1,0:T(8,128)(2,1)}, u32[]{:S(2)}) copy-start(bf16[384,768]{1,0:T(8,128)(2,1)} %all_gather.14) | copy-start | bytes 1769476
  (19 other events, 33.2 us)
